TPU v7x, 32 devices: a whole 2x2x4 slice. The times are simulated.
32 devices in a mesh: dp: 8 (over y, x, core), seq: 4 (over z).
Axes of the slice: x: 2, y: 2, z: 4, core: 2. Of those that a mesh axis runs over, the one named last changes fastest.
Arguments:
- block_input: bfloat16 [16, 512, 2048], P('dp', 'seq'), may hold values from -12 to 12
- segment_ids: int32 [16, 512], P('dp'), may hold values from 0 to 3, never falling along the last dimension, each value on 1 to 256 neighbouring positions
- cotangent: bfloat16 [16, 512, 2048], P('dp', 'seq'), may hold values from -6 to 6
- attn_gain: float32 [2048], P(('dp', 'seq')), may hold values from 0.5 to 1.5
- qkv_weight: float32 [2048, 3072], P('dp', 'seq'), may hold values from -1 to 1
- out_weight: float32 [2048, 2048], P('seq', 'dp'), may hold values from -0.75 to 0.75
- mlp_gain: float32 [2048], P(('dp', 'seq')), may hold values from 0.5 to 1.5
- gate_up_weight: float32 [2048, 2, 8192], P('dp', None, 'seq'), may hold values from -0.125 to 0.125
- down_weight: float32 [8192, 2048], P('seq', 'dp'), may hold values from -0.125 to 0.125
- first_attn_gain: float32 [2048], P(('dp', 'seq')), may hold values from -30 to 30
- first_qkv: float32 [2048, 3072], P('dp', 'seq'), may hold values from -30 to 30
- first_out: float32 [2048, 2048], P('seq', 'dp'), may hold values from -30 to 30
- first_mlp_gain: float32 [2048], P(('dp', 'seq')), may hold values from -30 to 30
- first_gate_up: float32 [2048, 2, 8192], P('dp', None, 'seq'), may hold values from -30 to 30
- first_down: float32 [8192, 2048], P('seq', 'dp'), may hold values from -30 to 30
- second_attn_gain: float32 [2048], P(('dp', 'seq')), may hold values from 100 to 300000
- second_qkv: float32 [2048, 3072], P('dp', 'seq'), may hold values from 100 to 30000
- second_out: float32 [2048, 2048], P('seq', 'dp'), may hold values from 50 to 500
- second_mlp_gain: float32 [2048], P(('dp', 'seq')), may hold values from 50 to 500
- second_gate_up: float32 [2048, 2, 8192], P('dp', None, 'seq'), may hold values from 50 to 500
- second_down: float32 [8192, 2048], P('seq', 'dp'), may hold values from 50 to 500
Outputs:
- output: bfloat16 [16, 512, 2048], P('dp', 'seq')
- input_grad: bfloat16 [16, 512, 2048], P('dp', 'seq')
- grad_attn_gain: float32 [2048], P(('dp', 'seq'))
- grad_qkv: float32 [2048, 3072], P('dp', 'seq')
- grad_out: float32 [2048, 2048], P('seq', 'dp')
- grad_mlp_gain: float32 [2048], P(('dp', 'seq'))
- grad_gate_up: float32 [2048, 2, 8192], P('dp', None, 'seq')
- grad_down: float32 [8192, 2048], P('seq', 'dp')
- new_attn_gain: float32 [2048], P(('dp', 'seq'))
- new_qkv: float32 [2048, 3072], P('dp', 'seq')
- new_out: float32 [2048, 2048], P('seq', 'dp')
- new_mlp_gain: float32 [2048], P(('dp', 'seq'))
- new_gate_up: float32 [2048, 2, 8192], P('dp', None, 'seq')
- new_down: float32 [8192, 2048], P('seq', 'dp')
- new_first_attn_gain: float32 [2048], P(('dp', 'seq'))
- new_first_qkv: float32 [2048, 3072], P('dp', 'seq')
- new_first_out: float32 [2048, 2048], P('seq', 'dp')
- new_first_mlp_gain: float32 [2048], P(('dp', 'seq'))
- new_first_gate_up: float32 [2048, 2, 8192], P('dp', None, 'seq')
- new_first_down: float32 [8192, 2048], P('seq', 'dp')
- new_second_attn_gain: float32 [2048], P(('dp', 'seq'))
- new_second_qkv: float32 [2048, 3072], P('dp', 'seq')
- new_second_out: float32 [2048, 2048], P('seq', 'dp')
- new_second_mlp_gain: float32 [2048], P(('dp', 'seq'))
- new_second_gate_up: float32 [2048, 2, 8192], P('dp', None, 'seq')
- new_second_down: float32 [8192, 2048], P('seq', 'dp')
Inputs may be any that keep to these rules, and one draw needn't show every extreme that they name: `segment_ids`: in each sequence the numbers never fall, and each segment holds 1 to 256 consecutive positions, one of them exactly that many.
All inputs are finite; a program needn't handle non-finite values.
Results may differ from a plain program's by a relative error of at most 0.023.
Values may be sent and summed in bfloat16 or wider, within the bound.
A program may use at most 320 MiB of HBM per device.

v0:
```python
import jax
import jax.numpy as jnp
from jax import lax
from jax.sharding import PartitionSpec as P

HEADS = 32
KV_HEADS = 8
HEAD_DIM = 64
norm_eps = 1e-05
rope_base = 500000.0
beta_one = 0.9
beta_two = 0.95
learn_rate = 0.01
weight_decay = 0.1
adam_eps = 1e-08
step_count = 10.0
masked_score = -1e30


def segment_positions(segments):
    length_here = segments.shape[-1]
    earlier = (segments[..., None, :] < segments[..., :, None]).astype(jnp.int32)
    return jnp.arange(length_here, dtype=jnp.int32) - jnp.sum(earlier, axis=-1, dtype=jnp.int32)


def rope_tables(positions, head_size):
    half_size = head_size // 2
    inverse = rope_base ** (-2.0 * jnp.arange(half_size, dtype=jnp.float32) / head_size)
    angles = positions.astype(jnp.float32)[..., None] * inverse
    return (jnp.cos(angles), jnp.sin(angles))


def rotate(vectors, cosine, sine):
    half_size = vectors.shape[-1] // 2
    first_half = vectors[..., :half_size]
    second_half = vectors[..., half_size:]
    cos_wide = cosine[..., None, :]
    sin_wide = sine[..., None, :]
    return jnp.concatenate(
        [
            first_half * cos_wide - second_half * sin_wide,
            second_half * cos_wide + first_half * sin_wide,
        ],
        -1,
    )


def unrotate(vectors, cosine, sine):
    half_size = vectors.shape[-1] // 2
    first_half = vectors[..., :half_size]
    second_half = vectors[..., half_size:]
    cos_wide = cosine[..., None, :]
    sin_wide = sine[..., None, :]
    return jnp.concatenate(
        [
            first_half * cos_wide + second_half * sin_wide,
            second_half * cos_wide - first_half * sin_wide,
        ],
        -1,
    )


def rms_forward(values, gain_wide):
    inverse = lax.rsqrt(jnp.mean(values * values, axis=-1, keepdims=True) + norm_eps)
    scaled = values * inverse
    return (scaled, inverse, (scaled * gain_wide).astype(jnp.bfloat16))


def rms_backward(d_normed, scaled, inverse, gain_wide):
    d_scaled = d_normed * gain_wide
    d_values = inverse * (d_scaled - scaled * jnp.mean(d_scaled * scaled, axis=-1, keepdims=True))
    return (d_values, jnp.sum(d_normed * scaled, axis=0))


def adam_update(weight, grad, first, second):
    new_first = beta_one * first + (1.0 - beta_one) * grad
    new_second = beta_two * second + (1.0 - beta_two) * grad * grad
    first_hat = new_first / (1.0 - beta_one**step_count)
    second_hat = new_second / (1.0 - beta_two**step_count)
    new_weight = weight - learn_rate * (
        first_hat / (jnp.sqrt(second_hat) + adam_eps) + weight_decay * weight
    )
    return (new_weight, new_first, new_second)


def contract_rows(left, right):
    return lax.dot_general(
        left, right, (((0,), (0,)), ((), ())), preferred_element_type=jnp.float32
    )


def times_transpose(left, right):
    return lax.dot_general(
        left, right, (((1,), (1,)), ((), ())), preferred_element_type=jnp.float32
    )


def per_device(
    block_input,
    segment_ids,
    cotangent,
    attn_gain,
    qkv_weight,
    out_weight,
    mlp_gain,
    gate_up_weight,
    down_weight,
    first_attn_gain,
    first_qkv,
    first_out,
    first_mlp_gain,
    first_gate_up,
    first_down,
    second_attn_gain,
    second_qkv,
    second_out,
    second_mlp_gain,
    second_gate_up,
    second_down,
):
    seqs_here, local_len, width = block_input.shape
    full_len = segment_ids.shape[1]
    total_rows = seqs_here * full_len
    groups = HEADS // KV_HEADS
    slot_count = groups + 2
    kv_local = qkv_weight.shape[1] // (slot_count * HEAD_DIM)
    query_cols = kv_local * groups * HEAD_DIM
    unit_count = down_weight.shape[0]
    score_scale = HEAD_DIM ** (-0.5)
    local_rows = seqs_here * local_len
    gain_pair = jnp.stack([attn_gain, mlp_gain]).astype(jnp.bfloat16)
    gain_block = lax.all_gather(gain_pair, ("dp", "seq"), axis=1, tiled=True)
    gain_one = gain_block[0].astype(jnp.float32)
    gain_two = gain_block[1].astype(jnp.float32)
    local_input = block_input.reshape(local_rows, width).astype(jnp.float32)
    scaled_one, inverse_one, normed_here = rms_forward(local_input, gain_one)
    normed_one = lax.all_gather(
        normed_here.reshape(seqs_here, local_len, width), "seq", axis=1, tiled=True
    ).reshape(total_rows, width)
    qkv_cols = lax.all_gather(qkv_weight.astype(jnp.bfloat16), "dp", axis=0, tiled=True)
    out_rows = lax.all_gather(out_weight.astype(jnp.bfloat16), "dp", axis=1, tiled=True)
    gate_up_cols = lax.all_gather(
        gate_up_weight.astype(jnp.bfloat16).reshape(-1, 2 * unit_count), "dp", axis=0, tiled=True
    )
    cot_all = lax.all_gather(cotangent, "seq", axis=1, tiled=True)
    down_rows = lax.all_gather(down_weight.astype(jnp.bfloat16), "dp", axis=1, tiled=True)
    positions = segment_positions(segment_ids)
    cosine, sine = rope_tables(positions, HEAD_DIM)
    index_line = jnp.arange(full_len, dtype=jnp.int32)
    allowed = (segment_ids[:, :, None] == segment_ids[:, None, :]) & (
        index_line[None, None, :] <= index_line[None, :, None]
    )
    allowed = allowed[:, None, None, :, :]
    qkv = jnp.dot(normed_one, qkv_cols, preferred_element_type=jnp.float32)
    qkv = qkv.reshape(seqs_here, full_len, kv_local, slot_count, HEAD_DIM)
    query = qkv[:, :, :, :groups].reshape(seqs_here, full_len, kv_local * groups, HEAD_DIM)
    query_groups = (
        rotate(query, cosine, sine)
        .astype(jnp.bfloat16)
        .reshape(seqs_here, full_len, kv_local, groups, HEAD_DIM)
    )
    key16 = rotate(qkv[:, :, :, groups], cosine, sine).astype(jnp.bfloat16)
    value16 = qkv[:, :, :, groups + 1].astype(jnp.bfloat16)

    def masked_scores():
        raw_scores = (
            jnp.einsum("sqgjd,skgd->sgjqk", query_groups, key16, preferred_element_type=jnp.float32)
            * score_scale
        )
        return jnp.where(allowed, raw_scores, masked_score)

    scores = masked_scores()
    top_score = jnp.max(scores, axis=-1, keepdims=True)
    log_total = top_score + jnp.log(jnp.sum(jnp.exp(scores - top_score), axis=-1, keepdims=True))
    probs16 = jnp.exp(scores - log_total).astype(jnp.bfloat16)
    attended16 = jnp.einsum(
        "sgjqk,skgd->sqgjd", probs16, value16, preferred_element_type=jnp.float32
    )
    attended16 = attended16.reshape(total_rows, query_cols).astype(jnp.bfloat16)
    attn_part = jnp.dot(attended16, out_rows, preferred_element_type=jnp.float32)

    def to_local(part):
        return (
            lax.psum_scatter(
                part.astype(jnp.bfloat16).reshape(seqs_here, full_len, width),
                "seq",
                scatter_dimension=1,
                tiled=True,
            )
            .astype(jnp.float32)
            .reshape(local_rows, width)
        )

    resid = local_input + to_local(attn_part)
    scaled_two, inverse_two, normed_two_here = rms_forward(resid, gain_two)
    normed_two = lax.all_gather(
        normed_two_here.reshape(seqs_here, local_len, width), "seq", axis=1, tiled=True
    ).reshape(total_rows, width)
    gate_up = jnp.dot(normed_two, gate_up_cols, preferred_element_type=jnp.float32)
    gate_part = gate_up[:, :unit_count]
    up_part = gate_up[:, unit_count:]
    sigmoid_gate = jax.nn.sigmoid(gate_part)
    active = gate_part * sigmoid_gate
    hidden16 = (active * up_part).astype(jnp.bfloat16)
    down_part = jnp.dot(hidden16, down_rows, preferred_element_type=jnp.float32)
    output = (resid + to_local(down_part)).astype(jnp.bfloat16).reshape(block_input.shape)
    cot_rows = cot_all.reshape(total_rows, width)
    d_hidden = times_transpose(cot_rows, down_rows)
    d_gate = d_hidden * up_part * sigmoid_gate * (1.0 + gate_part * (1.0 - sigmoid_gate))
    d_up = d_hidden * active
    d_gate_up16 = jnp.concatenate([d_gate, d_up], 1).astype(jnp.bfloat16)
    d_normed_two = to_local(times_transpose(d_gate_up16, gate_up_cols))
    down_term = contract_rows(cot_rows, hidden16)
    gate_up_term = contract_rows(normed_two, d_gate_up16)
    down_sum = lax.psum_scatter(
        down_term.astype(jnp.bfloat16), "dp", scatter_dimension=0, tiled=True
    ).astype(jnp.float32)
    grad_gate_up = (
        lax.psum_scatter(gate_up_term.astype(jnp.bfloat16), "dp", scatter_dimension=0, tiled=True)
        .reshape(gate_up_weight.shape)
        .astype(jnp.float32)
    )
    grad_down = down_sum.T
    resid_part, gain_two_term = rms_backward(d_normed_two, scaled_two, inverse_two, gain_two)
    d_resid = cotangent.reshape(local_rows, width).astype(jnp.float32) + resid_part
    d_resid16 = lax.all_gather(
        d_resid.astype(jnp.bfloat16).reshape(seqs_here, local_len, width), "seq", axis=1, tiled=True
    ).reshape(total_rows, width)
    d_attended = times_transpose(d_resid16, out_rows).astype(jnp.bfloat16)
    d_attended = d_attended.reshape(seqs_here, full_len, kv_local, groups, HEAD_DIM)
    scores = masked_scores()
    probs = jnp.exp(scores - log_total)
    d_probs = jnp.einsum(
        "sqgjd,skgd->sgjqk", d_attended, value16, preferred_element_type=jnp.float32
    )
    delta = jnp.sum(probs * d_probs, axis=-1, keepdims=True)
    d_scores16 = (probs * (d_probs - delta) * score_scale).astype(jnp.bfloat16)
    d_query = jnp.einsum("sgjqk,skgd->sqgjd", d_scores16, key16, preferred_element_type=jnp.float32)
    d_key = jnp.einsum(
        "sgjqk,sqgjd->skgd", d_scores16, query_groups, preferred_element_type=jnp.float32
    )
    d_value = jnp.einsum(
        "sgjqk,sqgjd->skgd", probs16, d_attended, preferred_element_type=jnp.float32
    )
    d_query = unrotate(
        d_query.reshape(seqs_here, full_len, kv_local * groups, HEAD_DIM), cosine, sine
    )
    d_query = d_query.reshape(seqs_here, full_len, kv_local, groups, HEAD_DIM)
    d_key = unrotate(d_key, cosine, sine)
    d_qkv16 = jnp.concatenate([d_query, d_key[:, :, :, None], d_value[:, :, :, None]], 3)
    d_qkv16 = d_qkv16.reshape(total_rows, qkv_cols.shape[1]).astype(jnp.bfloat16)
    d_normed_one = to_local(times_transpose(d_qkv16, qkv_cols))
    qkv_term = contract_rows(normed_one, d_qkv16)
    out_term = contract_rows(d_resid16, attended16)
    grad_qkv = lax.psum_scatter(
        qkv_term.astype(jnp.bfloat16), "dp", scatter_dimension=0, tiled=True
    ).astype(jnp.float32)
    out_sum = lax.psum_scatter(
        out_term.astype(jnp.bfloat16), "dp", scatter_dimension=0, tiled=True
    ).astype(jnp.float32)
    grad_out = out_sum.T
    input_part, gain_one_term = rms_backward(d_normed_one, scaled_one, inverse_one, gain_one)
    input_grad = (d_resid + input_part).astype(jnp.bfloat16).reshape(block_input.shape)
    gain_grads = lax.psum_scatter(
        jnp.stack([gain_one_term, gain_two_term], 1), ("dp", "seq"), scatter_dimension=0, tiled=True
    )
    grad_gain_one = gain_grads[:, 0]
    grad_gain_two = gain_grads[:, 1]
    w_one, m_one, v_one = adam_update(attn_gain, grad_gain_one, first_attn_gain, second_attn_gain)
    w_qkv, m_qkv, v_qkv = adam_update(qkv_weight, grad_qkv, first_qkv, second_qkv)
    w_out, m_out, v_out = adam_update(out_weight, grad_out, first_out, second_out)
    w_two, m_two, v_two = adam_update(mlp_gain, grad_gain_two, first_mlp_gain, second_mlp_gain)
    w_gu, m_gu, v_gu = adam_update(gate_up_weight, grad_gate_up, first_gate_up, second_gate_up)
    w_down, m_down, v_down = adam_update(down_weight, grad_down, first_down, second_down)
    return (
        output,
        input_grad,
        grad_gain_one,
        grad_qkv,
        grad_out,
        grad_gain_two,
        grad_gate_up,
        grad_down,
        w_one,
        w_qkv,
        w_out,
        w_two,
        w_gu,
        w_down,
        m_one,
        m_qkv,
        m_out,
        m_two,
        m_gu,
        m_down,
        v_one,
        v_qkv,
        v_out,
        v_two,
        v_gu,
        v_down,
    )


def solution(mesh):
    in_specs = (
        P("dp", "seq", None),
        P("dp", None),
        P("dp", "seq", None),
        P(("dp", "seq")),
        P("dp", "seq"),
        P("seq", "dp"),
        P(("dp", "seq")),
        P("dp", None, "seq"),
        P("seq", "dp"),
        P(("dp", "seq")),
        P("dp", "seq"),
        P("seq", "dp"),
        P(("dp", "seq")),
        P("dp", None, "seq"),
        P("seq", "dp"),
        P(("dp", "seq")),
        P("dp", "seq"),
        P("seq", "dp"),
        P(("dp", "seq")),
        P("dp", None, "seq"),
        P("seq", "dp"),
    )
    out_specs = (
        P("dp", "seq", None),
        P("dp", "seq", None),
        P(("dp", "seq")),
        P("dp", "seq"),
        P("seq", "dp"),
        P(("dp", "seq")),
        P("dp", None, "seq"),
        P("seq", "dp"),
        P(("dp", "seq")),
        P("dp", "seq"),
        P("seq", "dp"),
        P(("dp", "seq")),
        P("dp", None, "seq"),
        P("seq", "dp"),
        P(("dp", "seq")),
        P("dp", "seq"),
        P("seq", "dp"),
        P(("dp", "seq")),
        P("dp", None, "seq"),
        P("seq", "dp"),
        P(("dp", "seq")),
        P("dp", "seq"),
        P("seq", "dp"),
        P(("dp", "seq")),
        P("dp", None, "seq"),
        P("seq", "dp"),
    )
    return jax.shard_map(
        per_device, mesh=mesh, in_specs=in_specs, out_specs=out_specs, check_vma=False
    )
```

profile of v0, /device:TPU:0, one launch (start us, length us, event | category | flops | bytes accessed | tf_op | source)
XLA Modules:
  0.0 1514.0 jit_solution(13102967327842110868)
XLA Ops:
  10.0 69.8 %all-gather = bf16[32,64,2]{1,2,0:T(2,128)(2,1)S(1)} all-gather(bf16[1,64,2]{1,2,0:T(2,128)(2,1)S(1)} %maximum_bitcast_fusion.4), channel_id=1, replica_groups=mesh['dp'=8,'seq'=4] {'dp','seq'}, dimensions={0}, use_global_device_ids=true | all-gather | bytes 8448 | tf_op jit(solution)/shard_map/all_gather | solution.py:132
  91.1 70.0 %all-gather.10.cloned.1.call-done = bf16[2,512,2048]{2,1,0:T(8,128)(2,1)} async-done(((bf16[2,128,2048]{2,1,0:T(8,128)(2,1)}), bf16[2,512,2048]{2,1,0:T(8,128)(2,1)}) %all-gather.10.cloned.1.call-update) | async-done | bytes 4194320 | tf_op jit(solution)/shard_map/all_gather | solution.py:137
  169.2 7.4 fusion.5
  176.6 9.6 exponential_reduce_fusion
  186.2 10.3 fusion.35
  204.3 75.1 %reduce-scatter.12.cloned.1.call-done = bf16[2,128,2048]{2,1,0:T(8,128)(2,1)} async-done(((bf16[2,512,2048]{2,1,0:T(8,128)(2,1)}), bf16[2,128,2048]{2,1,0:T(8,128)(2,1)}) %reduce-scatter.12.cloned.1.call-update) | async-done | bytes 1048592 | tf_op jit(solution)/shard_map/reduce_scatter | solution.py:184
  292.1 72.9 %all-gather.16.cloned.1.call-done = bf16[2,512,2048]{2,1,0:T(8,128)(2,1)} async-done(((bf16[2,128,2048]{2,1,0:T(8,128)(2,1)}), bf16[2,512,2048]{2,1,0:T(8,128)(2,1)}) %all-gather.16.cloned.1.call-update) | async-done | bytes 4194320 | tf_op jit(solution)/shard_map/all_gather | solution.py:196
  365.0 90.6 %all-gather.18.cloned.1.call-done = bf16[2048,4096]{1,0:T(8,128)(2,1)} async-done(((bf16[256,4096]{1,0:T(8,128)(2,1)}), bf16[2048,4096]{1,0:T(8,128)(2,1)}) %all-gather.18.cloned.1.call-update) | async-done | bytes 16777232 | tf_op jit(solution)/shard_map/all_gather | solution.py:142
  455.6 23.9 %fusion.71 = f32[1024,4096]{1,0:T(8,128)} fusion(bf16[1024,2048]{1,0:T(8,128)(2,1)} %bitcast.221, bf16[2048,4096]{1,0:T(8,128)(2,1)} %all-gather.18.cloned.1.call-done), kind=kOutput, calls=%fused_computation.139 | convolution fusion | flops 17179869184 | bytes 37748736 | tf_op jit(solution)/shard_map/dot_general | solution.py:199
  479.5 58.4 %all-gather.22.cloned.1.call-done = bf16[2,512,2048]{2,1,0:T(8,128)(2,1)} async-done(((bf16[2,128,2048]{2,1,0:T(8,128)(2,1)}), bf16[2,512,2048]{2,1,0:T(8,128)(2,1)}) %all-gather.22.cloned.1.call-update) | async-done | bytes 4194320 | tf_op jit(solution)/shard_map/all_gather | solution.py:145
  538.0 56.8 %all-gather.20.cloned.1.call-done = bf16[2048,2048]{1,0:T(8,128)(2,1)} async-done(((bf16[2048,256]{1,0:T(8,128)(2,1)}), bf16[2048,2048]{1,0:T(8,128)(2,1)}) %all-gather.20.cloned.1.call-update) | async-done | bytes 8388624 | tf_op jit(solution)/shard_map/all_gather | solution.py:146
  594.8 21.7 %multiply_convert_fusion.1 = (bf16[1024,2048]{1,0:T(8,128)(2,1)}, bf16[1024,2048]{1,0:T(8,128)(2,1)}, bf16[1024,2048]{1,0:T(8,128)(2,1)}) fusion(f32[1024,4096]{1,0:T(8,128)} %fusion.71, bf16[1024,2048]{1,0:T(8,128)(2,1)} %bitcast.223, bf16[2048,2048]{1,0:T(8,128)(2,1)} %all-gather.20.cloned.1.call-done), kind=kOutput, calls=%fused_computation.15 | convolution fusion | flops 8621391872 | bytes 41943040 | tf_op jit(solution)/shard_map/dot_general | solution.py:93
  616.5 23.8 %fusion.11 = bf16[1024,2048]{1,0:T(8,128)(2,1)} fusion(bf16[2048,4096]{1,0:T(8,128)(2,1)} %all-gather.18.cloned.1.call-done, bf16[1024,2048]{1,0:T(8,128)(2,1)} %get-tuple-element.129, bf16[1024,2048]{1,0:T(8,128)(2,1)} %get-tuple-element.128), kind=kOutput, calls=%fused_computation.26 | convolution fusion | flops 17198743552 | bytes 29360128 | tf_op jit(solution)/shard_map/dot_general | solution.py:93
  640.6 76.7 %reduce-scatter.16.cloned.1.call-done = bf16[2,128,2048]{2,1,0:T(8,128)(2,1)} async-done(((bf16[2,512,2048]{2,1,0:T(8,128)(2,1)}), bf16[2,128,2048]{2,1,0:T(8,128)(2,1)}) %reduce-scatter.16.cloned.1.call-update) | async-done | bytes 1048592 | tf_op jit(solution)/shard_map/reduce_scatter | solution.py:184
  722.7 81.3 %all-gather.24.cloned.1.call-done = bf16[2,512,2048]{2,1,0:T(8,128)(2,1)} async-done(((bf16[2,128,2048]{2,1,0:T(8,128)(2,1)}), bf16[2,512,2048]{2,1,0:T(8,128)(2,1)}) %all-gather.24.cloned.1.call-update) | async-done | bytes 4194320 | tf_op jit(solution)/shard_map/all_gather | solution.py:226
  818.9 9.5 fusion.42
  828.4 24.6 %fusion.18 = f32[2,2,64,4,512]{4,2,3,1,0:T(8,128)} fusion(f32[2,2,512,512,4]{3,2,4,1,0:T(8,128)} %fusion.42, f32[2,2,512,512,4]{3,2,4,1,0:T(8,128)} %get-tuple-element.148, f32[2,2,4,512]{3,2,1,0:T(4,128)S(1)} %bitcast.215, pred[2,512,512]{1,2,0:T(8,128)(4,1)} %copy-done.10, bf16[2,512,2,32]{1,3,2,0:T(8,128)(2,1)S(1)} %get-tuple-element.140, ...), kind=kOutput, calls=%fused_computation.42 | convolution fusion | flops 583541248 | bytes 36470784 | tf_op jit(solution)/shard_map/sgjqk,skgd->sqgjd/dot_general | solution.py:238
  853.0 24.9 %fusion.36 = f32[2,512,2,64]{1,3,2,0:T(8,128)} fusion(f32[2,2,512,512,4]{3,2,4,1,0:T(8,128)} %fusion.42, f32[2,2,512,512,4]{3,2,4,1,0:T(8,128)} %get-tuple-element.148, f32[2,2,4,512]{3,2,1,0:T(4,128)S(1)} %bitcast.216, pred[2,512,512]{1,2,0:T(8,128)(4,1)} %copy-done.10, bf16[2,512,2,4,32]{1,4,3,2,0:T(8,128)(2,1)} %bitcast.201, ...), kind=kOutput, calls=%fused_computation.75 | convolution fusion | flops 585114112 | bytes 35684352 | tf_op jit(solution)/shard_map/sgjqk,sqgjd->skgd/dot_general | solution.py:239
  877.9 10.3 convolution_bitcast_fusion
  902.2 14.5 convert_bitcast_fusion
  923.1 7.9 convolution_convert_fusion.4
  931.1 14.0 convolution_convert_fusion.1
  945.2 32.4 %reduce-scatter.18.cloned.1.call-done = bf16[2,128,2048]{2,1,0:T(8,128)(2,1)} async-done(((bf16[2,512,2048]{2,1,0:T(8,128)(2,1)}), bf16[2,128,2048]{2,1,0:T(8,128)(2,1)}) %reduce-scatter.18.cloned.1.call-update) | async-done | bytes 1048592 | tf_op jit(solution)/shard_map/reduce_scatter | solution.py:184
  981.0 25.4 %convolution_convert_fusion = bf16[2048,4096]{1,0:T(8,128)(2,1)} fusion(bf16[1024,2048]{1,0:T(8,128)(2,1)} %bitcast.222, bf16[1024,2048]{1,0:T(8,128)(2,1)} %get-tuple-element.129, bf16[1024,2048]{1,0:T(8,128)(2,1)} %get-tuple-element.128), kind=kOutput, calls=%fused_computation.9 | convolution fusion | flops 17205035008 | bytes 29360128 | tf_op jit(solution)/shard_map/dot_general | solution.py:87
  1012.7 40.1 %reduce-scatter.26.cloned.1.call-done = bf16[256,2048]{0,1:T(8,128)(2,1)} async-done(((bf16[2048,2048]{0,1:T(8,128)(2,1)}), bf16[256,2048]{0,1:T(8,128)(2,1)}) %reduce-scatter.26.cloned.1.call-update) | async-done | bytes 1048592 | tf_op jit(solution)/shard_map/reduce_scatter | solution.py:215
  1052.8 6.9 multiply_subtract_fusion.1
  1059.6 37.5 %reduce-scatter.22.cloned.1.call-done = bf16[256,512]{1,0:T(8,128)(2,1)} async-done(((bf16[2048,512]{1,0:T(8,128)(2,1)}), bf16[256,512]{1,0:T(8,128)(2,1)}) %reduce-scatter.22.cloned.1.call-update) | async-done | bytes 262160 | tf_op jit(solution)/shard_map/reduce_scatter | solution.py:258
  1109.1 37.4 %reduce-scatter.20.cloned.1.call-done = bf16[256,768]{1,0:T(8,128)(2,1)} async-done(((bf16[2048,768]{1,0:T(8,128)(2,1)}), bf16[256,768]{1,0:T(8,128)(2,1)}) %reduce-scatter.20.cloned.1.call-update) | async-done | bytes 393232 | tf_op jit(solution)/shard_map/reduce_scatter | solution.py:255
  1150.1 75.4 %reduce-scatter.14.cloned.1.call-done = bf16[2,128,2048]{2,1,0:T(8,128)(2,1)} async-done(((bf16[2,512,2048]{2,1,0:T(8,128)(2,1)}), bf16[2,128,2048]{2,1,0:T(8,128)(2,1)}) %reduce-scatter.14.cloned.1.call-update) | async-done | bytes 1048592 | tf_op jit(solution)/shard_map/reduce_scatter | solution.py:184
  1230.4 135.3 %reduce-scatter.28.cloned.1.call-done = f32[64,2]{1,0:T(8,128)} async-done(((f32[2048,2]{1,0:T(8,128)}), f32[64,2]{1,0:T(8,128)}) %reduce-scatter.28.cloned.1.call-update) | async-done | bytes 528
  1367.9 113.8 %reduce-scatter.24.cloned.1.call-done = bf16[256,4096]{1,0:T(8,128)(2,1)} async-done(((bf16[2048,4096]{1,0:T(8,128)(2,1)}), bf16[256,4096]{1,0:T(8,128)(2,1)}) %reduce-scatter.24.cloned.1.call-update) | async-done | bytes 2097168 | tf_op jit(solution)/shard_map/reduce_scatter | solution.py:219
  1488.3 18.9 %multiply_subtract_fusion = (f32[256,2,2048]{2,1,0:T(2,128)}, f32[256,2,2048]{2,1,0:T(2,128)}, f32[256,2,2048]{2,1,0:T(2,128)}) fusion(f32[256,2,2048]{2,1,0:T(2,128)} %param.28, f32[256,2,2048]{2,1,0:T(2,128)} %reshape.336, f32[256,2,2048]{2,1,0:T(2,128)} %param.34, f32[256,2,2048]{2,1,0:T(2,128)} %param.40), kind=kLoop, calls=%fused_computation.24 | loop fusion | flops 15728640 | bytes 29360128 | tf_op jit(solution)/shard_map/sub | solution.py:80
  (170 shorter events, 121.8 us)
Async XLA Ops:
  7.2 76.8 %copy-start.11 = (f32[512,256]{1,0:T(8,128)S(1)}, f32[512,256]{1,0:T(8,128)}, u32[]{:S(2)}) copy-start(f32[512,256]{1,0:T(8,128)} %param.26) | copy-start | bytes 1572868
  7.2 77.8 %copy-start.21 = (s32[2,512]{1,0:T(2,128)S(1)}, s32[2,512]{1,0:T(2,128)}, u32[]{:S(2)}) copy-start(s32[2,512]{1,0:T(2,128)} %param.22) | copy-start | bytes 12292
  7.2 79.1 %all-gather.12.cloned.1.call-start = ((), (), s32[]{:S(2)}) async-start(), calls=%async_computation.10 | async-start | bytes 3538944 | tf_op jit(solution)/shard_map/all_gather | solution.py:140
  9.3 151.9 %all-gather.10.cloned.1.call-start = ((), (), s32[]{:S(2)}) async-start(), calls=%async_computation.9 | async-start | bytes 5242880 | tf_op jit(solution)/shard_map/all_gather | solution.py:137
  84.0 113.9 %all-gather.14.cloned.1.call-start = ((), (), s32[]{:S(2)}) async-start(), calls=%async_computation.11 | async-start | bytes 2359296 | tf_op jit(solution)/shard_map/all_gather | solution.py:141
  84.8 194.6 %reduce-scatter.12.cloned.1.call-start = ((), (), s32[]{:S(2)}) async-start(), calls=%async_computation.12 | async-start | bytes 5242880 | tf_op jit(solution)/shard_map/reduce_scatter | solution.py:184
  85.7 100.4 %copy-start.10 = (pred[2,512,512]{1,2,0:T(8,128)(4,1)}, pred[2,512,512]{1,2,0:T(8,128)(4,1)S(1)}, u32[]{:S(2)}) copy-start(pred[2,512,512]{1,2,0:T(8,128)(4,1)S(1)} %compare_and_fusion) | copy-start | bytes 1572868
  86.3 81.5 %copy-start.4 = (f32[2,512,32]{1,2,0:T(8,128)}, f32[2,512,32]{1,2,0:T(8,128)S(1)}, u32[]{:S(2)}) copy-start(f32[2,512,32]{1,2,0:T(8,128)S(1)} %get-tuple-element.145) | copy-start | bytes 393220
  86.3 81.5 %copy-start.6 = (f32[2,512,32]{1,2,0:T(8,128)}, f32[2,512,32]{1,2,0:T(8,128)S(1)}, u32[]{:S(2)}) copy-start(f32[2,512,32]{1,2,0:T(8,128)S(1)} %get-tuple-element.146) | copy-start | bytes 393220
  204.3 160.8 %all-gather.16.cloned.1.call-start = ((), (), s32[]{:S(2)}) async-start(), calls=%async_computation.13 | async-start | bytes 5242880 | tf_op jit(solution)/shard_map/all_gather | solution.py:196
  283.7 172.0 %all-gather.18.cloned.1.call-start = ((), (), s32[]{:S(2)}) async-start(), calls=%async_computation.14 | async-start | bytes 18874368 | tf_op jit(solution)/shard_map/all_gather | solution.py:142
  290.2 247.8 %all-gather.22.cloned.1.call-start = ((), (), s32[]{:S(2)}) async-start(), calls=%async_computation.17 | async-start | bytes 5242880 | tf_op jit(solution)/shard_map/all_gather | solution.py:145
  290.9 303.9 %all-gather.20.cloned.1.call-start = ((), (), s32[]{:S(2)}) async-start(), calls=%async_computation.15 | async-start | bytes 9437184 | tf_op jit(solution)/shard_map/all_gather | solution.py:146
  292.1 425.2 %reduce-scatter.16.cloned.1.call-start = ((), (), s32[]{:S(2)}) async-start(), calls=%async_computation.18 | async-start | bytes 5242880 | tf_op jit(solution)/shard_map/reduce_scatter | solution.py:184
  640.3 77.0 %copy-start.1 = (bf16[2,128,2048]{2,1,0:T(8,128)(2,1)S(1)}, bf16[2,128,2048]{2,1,0:T(8,128)(2,1)}, u32[]{:S(2)}) copy-start(bf16[2,128,2048]{2,1,0:T(8,128)(2,1)} %reduce-scatter.12.cloned.1.call-done) | copy-start | bytes 3145732
  640.3 79.0 %copy-start.2 = (bf16[2,128,2048]{2,1,0:T(8,128)(2,1)S(1)}, bf16[2,128,2048]{2,1,0:T(8,128)(2,1)}, u32[]{:S(2)}) copy-start(bf16[2,128,2048]{2,1,0:T(8,128)(2,1)} %param.23) | copy-start | bytes 3145732
  640.4 163.6 %all-gather.24.cloned.1.call-start = ((), (), s32[]{:S(2)}) async-start(), calls=%async_computation.19 | async-start | bytes 5242880 | tf_op jit(solution)/shard_map/all_gather | solution.py:226
  722.6 255.0 %reduce-scatter.18.cloned.1.call-start = ((), (), s32[]{:S(2)}) async-start(), calls=%async_computation.20 | async-start | bytes 5242880 | tf_op jit(solution)/shard_map/reduce_scatter | solution.py:184
  902.2 150.6 %reduce-scatter.26.cloned.1.call-start = ((), (), s32[]{:S(2)}) async-start(), calls=%async_computation.24 | async-start | bytes 9437184 | tf_op jit(solution)/shard_map/reduce_scatter | solution.py:215
  916.8 180.4 %reduce-scatter.22.cloned.1.call-start = ((), (), s32[]{:S(2)}) async-start(), calls=%async_computation.22 | async-start | bytes 2359296 | tf_op jit(solution)/shard_map/reduce_scatter | solution.py:258
  923.0 223.5 %reduce-scatter.20.cloned.1.call-start = ((), (), s32[]{:S(2)}) async-start(), calls=%async_computation.21 | async-start | bytes 3538944 | tf_op jit(solution)/shard_map/reduce_scatter | solution.py:255
  931.0 294.5 %reduce-scatter.14.cloned.1.call-start = ((), (), s32[]{:S(2)}) async-start(), calls=%async_computation.16 | async-start | bytes 5242880 | tf_op jit(solution)/shard_map/reduce_scatter | solution.py:184
  945.1 420.6 %reduce-scatter.28.cloned.1.call-start = ((), (), s32[]{:S(2)}) async-start(), calls=%async_computation.25 | async-start | bytes 1081344
  981.0 500.8 %reduce-scatter.24.cloned.1.call-start = ((), (), s32[]{:S(2)}) async-start(), calls=%async_computation.23 | async-start | bytes 18874368 | tf_op jit(solution)/shard_map/reduce_scatter | solution.py:219
  1150.0 216.7 %copy-start.26 = (f32[64]{0:T(128)S(1)}, f32[64]{0:T(128)}, u32[]{:S(2)}) copy-start(f32[64]{0:T(128)} %param.27) | copy-start | bytes 772
  1150.0 216.7 %copy-start.28 = (f32[64]{0:T(128)S(1)}, f32[64]{0:T(128)}, u32[]{:S(2)}) copy-start(f32[64]{0:T(128)} %param.33) | copy-start | bytes 772
  1150.0 216.7 %copy-start.29 = (f32[64]{0:T(128)S(1)}, f32[64]{0:T(128)}, u32[]{:S(2)}) copy-start(f32[64]{0:T(128)} %param.39) | copy-start | bytes 772
  1150.0 217.3 %copy-start.27 = (f32[64]{0:T(128)S(1)}, f32[64]{0:T(128)}, u32[]{:S(2)}) copy-start(f32[64]{0:T(128)} %param.24) | copy-start | bytes 772
  1150.1 217.3 %copy-start.30 = (f32[64]{0:T(128)S(1)}, f32[64]{0:T(128)}, u32[]{:S(2)}) copy-start(f32[64]{0:T(128)} %param.30) | copy-start | bytes 772
  1150.1 217.3 %copy-start.31 = (f32[64]{0:T(128)S(1)}, f32[64]{0:T(128)}, u32[]{:S(2)}) copy-start(f32[64]{0:T(128)} %param.36) | copy-start | bytes 772
  1366.7 140.5 %copy-start.24 = (f32[64,1]{0,1:T(1,128)}, f32[64,1]{0,1:T(1,128)S(1)}, u32[]{:S(2)}) copy-start(f32[64,1]{0,1:T(1,128)S(1)} %copy.120) | copy-start | bytes 772
  1366.8 140.4 %copy-start.25 = (f32[64,1]{0,1:T(1,128)}, f32[64,1]{0,1:T(1,128)S(1)}, u32[]{:S(2)}) copy-start(f32[64,1]{0,1:T(1,128)S(1)} %copy.119) | copy-start | bytes 772
  (17 other events, 227.6 us)
Sparse Core Ops, SparseCore 0:
  10.5 34.9 all-gather.11
  84.1 76.9 all-gather.9
  163.6 26.5 all-gather.13
  204.4 74.9 reduce-scatter.11
  283.8 81.2 all-gather.15
  367.4 88.2 all-gather.17
  457.2 80.7 all-gather.21
  540.4 54.3 all-gather.19
  640.5 76.7 reduce-scatter.15
  722.7 81.2 all-gather.23
  902.3 75.2 reduce-scatter.17
  980.9 71.7 reduce-scatter.25
  1056.1 41.0 reduce-scatter.21
  1100.4 46.0 reduce-scatter.19
  1148.6 76.7 reduce-scatter.13
  1228.1 137.5 reduce-scatter.27
  1369.1 112.5 reduce-scatter.23
where the time goes:
time: 1520 us; the launch traced here: 1510 us
  waiting for transfers between devices  1050 us (69%)
  matrix products  248 us (16%)
  other arithmetic  81.3 us (5%)
  blocking collectives  69.8 us (5%)
  local copies, waits for them, and re-layouts  43.9 us (3%)
    reduce_scatter x4, waiting for transfers between devices, to_local(): lax.psum_scatter(part.astype(jnp.bfloat16).reshape(seqs_here, full_len, w...  260 us
    unnamed x18, waiting for transfers between devices  136 us
    reduce_scatter x1, waiting for transfers between devices, per_device(): lax.psum_scatter(gate_up_term.astype(jnp.bfloat16), 'dp', scatter_dimensi...  114 us
    all_gather x1, waiting for transfers between devices, per_device(): lax.all_gather(gate_up_weight.astype(jnp.bfloat16).reshape(-1, 2 * unit_c...  90.6 us
    all_gather x1, waiting for transfers between devices, per_device(): lax.all_gather(d_resid.astype(jnp.bfloat16).reshape(seqs_here, local_len,...  81.3 us
    all_gather x1, waiting for transfers between devices, per_device(): lax.all_gather(normed_two_here.reshape(seqs_here, local_len, width), 'seq...  72.9 us
    all_gather x1, waiting for transfers between devices, per_device(): lax.all_gather(normed_here.reshape(seqs_here, local_len, width), 'seq', a...  70 us
    all_gather x1, blocking collectives, per_device(): gain_block = lax.all_gather(gain_pair, ('dp', 'seq'), axis=1, tiled=True)  69.8 us
  transfers between devices with their start and end apart: 17, of which 15 were waited for; matrix products, arithmetic and copies ran while one was open for 12% of the time, Pallas kernels for 0%

commit v1 on v0

--- a/solution.py
+++ b/solution.py
@@ -139,8 +139,17 @@
     ).reshape(total_rows, width)
     qkv_cols = lax.all_gather(qkv_weight.astype(jnp.bfloat16), "dp", axis=0, tiled=True)
     out_rows = lax.all_gather(out_weight.astype(jnp.bfloat16), "dp", axis=1, tiled=True)
-    gate_up_cols = lax.all_gather(
-        gate_up_weight.astype(jnp.bfloat16).reshape(-1, 2 * unit_count), "dp", axis=0, tiled=True
+    gate_up_cols = jnp.concatenate(
+        lax.all_to_all(
+            jnp.stack(
+                [gate_up_weight.astype(jnp.bfloat16).reshape(-1, 2 * unit_count)]
+                * lax.axis_size("dp")
+            ),
+            "dp",
+            0,
+            0,
+        ),
+        axis=0,
     )
     cot_all = lax.all_gather(cotangent, "seq", axis=1, tiled=True)
     down_rows = lax.all_gather(down_weight.astype(jnp.bfloat16), "dp", axis=1, tiled=True)

time: 1520 us -> 1450 us (0.954)
  waiting for transfers between devices: 1050 us -> 978 us
    all_to_all x0 -> x1, waiting for transfers between devices: none -> 203 us  [per_device(): lax.all_to_all(jnp.stack([gate_up_weight.astype(jnp.bfloat16).reshape(-1,...]
    all_gather x1 -> x0, waiting for transfers between devices: 90.6 us -> none  [per_device(): lax.all_gather(gate_up_weight.astype(jnp.bfloat16).reshape(-1, 2 * unit_c...]
    all_gather x1, waiting for transfers between devices: 72.9 us -> 0.01 us  [per_device(): lax.all_gather(normed_two_here.reshape(seqs_here, local_len, width), 'seq...]
    all_gather x1, waiting for transfers between devices: 58.4 us -> 0.01 us  [per_device(): cot_all = lax.all_gather(cotangent, 'seq', axis=1, tiled=True)]
    all_gather x1, waiting for transfers between devices: 56.8 us -> 0.01 us  [per_device(): lax.all_gather(down_weight.astype(jnp.bfloat16), 'dp', axis=1, tiled=True)]
    unnamed x18 -> x17, waiting for transfers between devices: 136 us -> 136 us
  transfers between devices with their start and end apart: 17 -> 17, of which waited for: 15 -> 12; matrix products, arithmetic and copies ran while one was open for 12% -> 13% of each run, Pallas kernels for 0% -> 0%
where the time goes in v1:
time: 1450 us
  waiting for transfers between devices  978 us (67%)
  matrix products  248 us (17%)
  other arithmetic  81.3 us (6%)
  blocking collectives  69.8 us (5%)
  local copies, waits for them, and re-layouts  49.1 us (3%)
  between operations  14.8 us (1%)
    reduce_scatter x4, waiting for transfers between devices, to_local(): lax.psum_scatter(part.astype(jnp.bfloat16).reshape(seqs_here, full_len, w...  259 us
    all_to_all x1, waiting for transfers between devices, per_device(): lax.all_to_all(jnp.stack([gate_up_weight.astype(jnp.bfloat16).reshape(-1,...  203 us
    unnamed x17, waiting for transfers between devices  136 us
    reduce_scatter x1, waiting for transfers between devices, per_device(): lax.psum_scatter(gate_up_term.astype(jnp.bfloat16), 'dp', scatter_dimensi...  114 us
    all_gather x1, waiting for transfers between devices, per_device(): lax.all_gather(d_resid.astype(jnp.bfloat16).reshape(seqs_here, local_len,...  81.3 us
    all_gather x1, waiting for transfers between devices, per_device(): lax.all_gather(normed_here.reshape(seqs_here, local_len, width), 'seq', a...  70 us
    all_gather x1, blocking collectives, per_device(): gain_block = lax.all_gather(gain_pair, ('dp', 'seq'), axis=1, tiled=True)  69.8 us
    dot_general x4, matrix products, times_transpose(): lax.dot_general(left, right, (((1,), (1,)), ((), ())), preferred_element_...  56.8 us
  transfers between devices with their start and end apart: 17, of which 12 were waited for; matrix products, arithmetic and copies ran while one was open for 13% of the time, Pallas kernels for 0%

profile of v1, /device:TPU:0, one launch (start us, length us, event | category | flops | bytes accessed | tf_op | source)
XLA Modules:
  0.0 1447.9 jit_solution(8882844299108043412)
XLA Ops:
  10.0 69.8 %all-gather = bf16[32,64,2]{1,2,0:T(2,128)(2,1)S(1)} all-gather(bf16[1,64,2]{1,2,0:T(2,128)(2,1)S(1)} %maximum_bitcast_fusion.4), channel_id=1, replica_groups=mesh['dp'=8,'seq'=4] {'dp','seq'}, dimensions={0}, use_global_device_ids=true | all-gather | bytes 8448 | tf_op jit(solution)/shard_map/all_gather | solution.py:132
  91.1 70.0 %all-gather.9.cloned.1.call-done = bf16[2,512,2048]{2,1,0:T(8,128)(2,1)} async-done(((bf16[2,128,2048]{2,1,0:T(8,128)(2,1)}), bf16[2,512,2048]{2,1,0:T(8,128)(2,1)}) %all-gather.9.cloned.1.call-update) | async-done | bytes 4194320 | tf_op jit(solution)/shard_map/all_gather | solution.py:137
  169.2 7.4 fusion.5
  176.6 9.6 exponential_reduce_fusion
  186.2 10.3 fusion.35
  197.9 6.4 convolution_convert_fusion.2
  204.7 74.7 %reduce-scatter.12.cloned.1.call-done = bf16[2,128,2048]{2,1,0:T(8,128)(2,1)} async-done(((bf16[2,512,2048]{2,1,0:T(8,128)(2,1)}), bf16[2,128,2048]{2,1,0:T(8,128)(2,1)}) %reduce-scatter.12.cloned.1.call-update) | async-done | bytes 1048592 | tf_op jit(solution)/shard_map/reduce_scatter | solution.py:193
  289.3 6.5 stack.27
  303.0 202.6 %all-to-all-done = bf16[8,256,4096]{2,1,0:T(8,128)(2,1)} async-done(((bf16[8,256,4096]{2,1,0:T(8,128)(2,1)}), bf16[8,256,4096]{2,1,0:T(8,128)(2,1)}, u32[]{:S(2)}, u32[]{:S(2)}) %all-to-all-start) | async-done | bytes 16777248 | tf_op jit(solution)/shard_map/all_to_all | solution.py:143
  505.6 23.4 %fusion.71 = f32[1024,4096]{1,0:T(8,128)} fusion(bf16[1024,2048]{1,0:T(8,128)(2,1)} %bitcast.222, bf16[2048,4096]{1,0:T(8,128)(2,1)} %bitcast.25), kind=kOutput, calls=%fused_computation.139 | convolution fusion | flops 17179869184 | bytes 37748736 | tf_op jit(solution)/shard_map/dot_general | solution.py:208
  529.0 21.8 %multiply_convert_fusion.1 = (bf16[1024,2048]{1,0:T(8,128)(2,1)}, bf16[1024,2048]{1,0:T(8,128)(2,1)}, bf16[1024,2048]{1,0:T(8,128)(2,1)}) fusion(f32[1024,4096]{1,0:T(8,128)} %fusion.71, bf16[1024,2048]{1,0:T(8,128)(2,1)} %bitcast.224, bf16[2048,2048]{1,0:T(8,128)(2,1)} %all-gather.17.cloned.1.call-done), kind=kOutput, calls=%fused_computation.15 | convolution fusion | flops 8621391872 | bytes 41943040 | tf_op jit(solution)/shard_map/dot_general | solution.py:93
  550.8 23.8 %fusion.11 = bf16[1024,2048]{1,0:T(8,128)(2,1)} fusion(bf16[2048,4096]{1,0:T(8,128)(2,1)} %bitcast.25, bf16[1024,2048]{1,0:T(8,128)(2,1)} %get-tuple-element.129, bf16[1024,2048]{1,0:T(8,128)(2,1)} %get-tuple-element.128), kind=kOutput, calls=%fused_computation.26 | convolution fusion | flops 17198743552 | bytes 29360128 | tf_op jit(solution)/shard_map/dot_general | solution.py:93
  574.8 76.1 %reduce-scatter.16.cloned.1.call-done = bf16[2,128,2048]{2,1,0:T(8,128)(2,1)} async-done(((bf16[2,512,2048]{2,1,0:T(8,128)(2,1)}), bf16[2,128,2048]{2,1,0:T(8,128)(2,1)}) %reduce-scatter.16.cloned.1.call-update) | async-done | bytes 1048592 | tf_op jit(solution)/shard_map/reduce_scatter | solution.py:193
  656.3 81.3 %all-gather.21.cloned.1.call-done = bf16[2,512,2048]{2,1,0:T(8,128)(2,1)} async-done(((bf16[2,128,2048]{2,1,0:T(8,128)(2,1)}), bf16[2,512,2048]{2,1,0:T(8,128)(2,1)}) %all-gather.21.cloned.1.call-update) | async-done | bytes 4194320 | tf_op jit(solution)/shard_map/all_gather | solution.py:235
  752.5 9.5 fusion.42
  762.0 24.6 %fusion.18 = f32[2,2,64,4,512]{4,2,3,1,0:T(8,128)} fusion(f32[2,2,512,512,4]{3,2,4,1,0:T(8,128)} %fusion.42, f32[2,2,512,512,4]{3,2,4,1,0:T(8,128)} %get-tuple-element.148, f32[2,2,4,512]{3,2,1,0:T(4,128)S(1)} %bitcast.216, pred[2,512,512]{1,2,0:T(8,128)(4,1)} %copy-done.10, bf16[2,512,2,32]{1,3,2,0:T(8,128)(2,1)S(1)} %copy-done.22, ...), kind=kOutput, calls=%fused_computation.42 | convolution fusion | flops 583541248 | bytes 36470784 | tf_op jit(solution)/shard_map/sgjqk,skgd->sqgjd/dot_general | solution.py:247
  786.7 24.9 %fusion.36 = f32[2,512,2,64]{1,3,2,0:T(8,128)} fusion(f32[2,2,512,512,4]{3,2,4,1,0:T(8,128)} %fusion.42, f32[2,2,512,512,4]{3,2,4,1,0:T(8,128)} %get-tuple-element.148, f32[2,2,4,512]{3,2,1,0:T(4,128)S(1)} %bitcast.217, pred[2,512,512]{1,2,0:T(8,128)(4,1)} %copy-done.10, bf16[2,512,2,4,32]{1,4,3,2,0:T(8,128)(2,1)} %bitcast.202, ...), kind=kOutput, calls=%fused_computation.75 | convolution fusion | flops 585114112 | bytes 35684352 | tf_op jit(solution)/shard_map/sgjqk,sqgjd->skgd/dot_general | solution.py:248
  811.6 10.3 convolution_bitcast_fusion
  835.9 14.5 %convert_bitcast_fusion = bf16[2048,2048]{0,1:T(8,128)(2,1)} fusion(bf16[1024,2048]{1,0:T(8,128)(2,1)} %get-tuple-element.130, bf16[1024,2048]{1,0:T(8,128)(2,1)} %bitcast.225), kind=kOutput, calls=%fused_computation.13 | convolution fusion | flops 8594128896 | bytes 16777216 | tf_op jit(solution)/shard_map/dot_general | solution.py:87
  856.8 7.9 convolution_convert_fusion.4
  864.8 14.0 convolution_convert_fusion.1
  878.9 32.4 %reduce-scatter.18.cloned.1.call-done = bf16[2,128,2048]{2,1,0:T(8,128)(2,1)} async-done(((bf16[2,512,2048]{2,1,0:T(8,128)(2,1)}), bf16[2,128,2048]{2,1,0:T(8,128)(2,1)}) %reduce-scatter.18.cloned.1.call-update) | async-done | bytes 1048592 | tf_op jit(solution)/shard_map/reduce_scatter | solution.py:193
  914.7 25.4 %convolution_convert_fusion = bf16[2048,4096]{1,0:T(8,128)(2,1)} fusion(bf16[1024,2048]{1,0:T(8,128)(2,1)} %bitcast.223, bf16[1024,2048]{1,0:T(8,128)(2,1)} %get-tuple-element.129, bf16[1024,2048]{1,0:T(8,128)(2,1)} %get-tuple-element.128), kind=kOutput, calls=%fused_computation.9 | convolution fusion | flops 17205035008 | bytes 29360128 | tf_op jit(solution)/shard_map/dot_general | solution.py:87
  946.4 40.2 %reduce-scatter.26.cloned.1.call-done = bf16[256,2048]{0,1:T(8,128)(2,1)} async-done(((bf16[2048,2048]{0,1:T(8,128)(2,1)}), bf16[256,2048]{0,1:T(8,128)(2,1)}) %reduce-scatter.26.cloned.1.call-update) | async-done | bytes 1048592 | tf_op jit(solution)/shard_map/reduce_scatter | solution.py:224
  986.6 6.9 multiply_subtract_fusion.1
  993.5 37.4 %reduce-scatter.22.cloned.1.call-done = bf16[256,512]{1,0:T(8,128)(2,1)} async-done(((bf16[2048,512]{1,0:T(8,128)(2,1)}), bf16[256,512]{1,0:T(8,128)(2,1)}) %reduce-scatter.22.cloned.1.call-update) | async-done | bytes 262160 | tf_op jit(solution)/shard_map/reduce_scatter | solution.py:267
  1042.8 37.6 %reduce-scatter.20.cloned.1.call-done = bf16[256,768]{1,0:T(8,128)(2,1)} async-done(((bf16[2048,768]{1,0:T(8,128)(2,1)}), bf16[256,768]{1,0:T(8,128)(2,1)}) %reduce-scatter.20.cloned.1.call-update) | async-done | bytes 393232 | tf_op jit(solution)/shard_map/reduce_scatter | solution.py:264
  1083.9 75.4 %reduce-scatter.14.cloned.1.call-done = bf16[2,128,2048]{2,1,0:T(8,128)(2,1)} async-done(((bf16[2,512,2048]{2,1,0:T(8,128)(2,1)}), bf16[2,128,2048]{2,1,0:T(8,128)(2,1)}) %reduce-scatter.14.cloned.1.call-update) | async-done | bytes 1048592 | tf_op jit(solution)/shard_map/reduce_scatter | solution.py:193
  1164.2 135.3 %reduce-scatter.28.cloned.1.call-done = f32[64,2]{1,0:T(8,128)} async-done(((f32[2048,2]{1,0:T(8,128)}), f32[64,2]{1,0:T(8,128)}) %reduce-scatter.28.cloned.1.call-update) | async-done | bytes 528
  1301.7 114.0 %reduce-scatter.24.cloned.1.call-done = bf16[256,4096]{1,0:T(8,128)(2,1)} async-done(((bf16[2048,4096]{1,0:T(8,128)(2,1)}), bf16[256,4096]{1,0:T(8,128)(2,1)}) %reduce-scatter.24.cloned.1.call-update) | async-done | bytes 2097168 | tf_op jit(solution)/shard_map/reduce_scatter | solution.py:228
  1415.7 6.6 reshape.338
  1422.2 18.9 %multiply_subtract_fusion = (f32[256,2,2048]{2,1,0:T(2,128)}, f32[256,2,2048]{2,1,0:T(2,128)}, f32[256,2,2048]{2,1,0:T(2,128)}) fusion(f32[256,2,2048]{2,1,0:T(2,128)} %param.28, f32[256,2,2048]{2,1,0:T(2,128)} %reshape.338, f32[256,2,2048]{2,1,0:T(2,128)} %param.34, f32[256,2,2048]{2,1,0:T(2,128)} %param.40), kind=kLoop, calls=%fused_computation.24 | loop fusion | flops 15728640 | bytes 29360128 | tf_op jit(solution)/shard_map/sub | solution.py:80
  (178 shorter events, 113.6 us)
Async XLA Ops:
  7.2 76.8 %copy-start.11 = (f32[512,256]{1,0:T(8,128)S(1)}, f32[512,256]{1,0:T(8,128)}, u32[]{:S(2)}) copy-start(f32[512,256]{1,0:T(8,128)} %param.26) | copy-start | bytes 1572868
  7.2 77.8 %copy-start.25 = (s32[2,512]{1,0:T(2,128)S(1)}, s32[2,512]{1,0:T(2,128)}, u32[]{:S(2)}) copy-start(s32[2,512]{1,0:T(2,128)} %param.22) | copy-start | bytes 12292
  7.2 79.1 %all-gather.11.cloned.1.call-start = ((), (), s32[]{:S(2)}) async-start(), calls=%async_computation.11 | async-start | bytes 3538944 | tf_op jit(solution)/shard_map/all_gather | solution.py:140
  9.3 151.9 %all-gather.9.cloned.1.call-start = ((), (), s32[]{:S(2)}) async-start(), calls=%async_computation.10 | async-start | bytes 5242880 | tf_op jit(solution)/shard_map/all_gather | solution.py:137
  84.0 113.9 %all-gather.13.cloned.1.call-start = ((), (), s32[]{:S(2)}) async-start(), calls=%async_computation.12 | async-start | bytes 2359296 | tf_op jit(solution)/shard_map/all_gather | solution.py:141
  84.8 194.6 %reduce-scatter.12.cloned.1.call-start = ((), (), s32[]{:S(2)}) async-start(), calls=%async_computation.13 | async-start | bytes 5242880 | tf_op jit(solution)/shard_map/reduce_scatter | solution.py:193
  85.7 100.4 %copy-start.10 = (pred[2,512,512]{1,2,0:T(8,128)(4,1)}, pred[2,512,512]{1,2,0:T(8,128)(4,1)S(1)}, u32[]{:S(2)}) copy-start(pred[2,512,512]{1,2,0:T(8,128)(4,1)S(1)} %compare_and_fusion) | copy-start | bytes 1572868
  86.3 81.6 %copy-start.4 = (f32[2,512,32]{1,2,0:T(8,128)}, f32[2,512,32]{1,2,0:T(8,128)S(1)}, u32[]{:S(2)}) copy-start(f32[2,512,32]{1,2,0:T(8,128)S(1)} %get-tuple-element.145) | copy-start | bytes 393220
  86.3 81.6 %copy-start.6 = (f32[2,512,32]{1,2,0:T(8,128)}, f32[2,512,32]{1,2,0:T(8,128)S(1)}, u32[]{:S(2)}) copy-start(f32[2,512,32]{1,2,0:T(8,128)S(1)} %get-tuple-element.146) | copy-start | bytes 393220
  204.3 301.3 %all-gather.15.cloned.1.call-start = ((), (), s32[]{:S(2)}) async-start(), calls=%async_computation.14 | async-start | bytes 5242880 | tf_op jit(solution)/shard_map/all_gather | solution.py:205
  283.7 245.3 %all-gather.19.cloned.1.call-start = ((), (), s32[]{:S(2)}) async-start(), calls=%async_computation.17 | async-start | bytes 5242880 | tf_op jit(solution)/shard_map/all_gather | solution.py:154
  295.9 209.7 %all-to-all-start = ((bf16[8,256,4096]{2,1,0:T(8,128)(2,1)}), bf16[8,256,4096]{2,1,0:T(8,128)(2,1)}, u32[]{:S(2)}, u32[]{:S(2)}) async-start(bf16[8,256,4096]{2,1,0:T(8,128)(2,1)} %stack.27), calls=%async_computation.1 | async-start | bytes 33554432 | tf_op jit(solution)/shard_map/all_to_all | solution.py:143
  301.8 227.2 %all-gather.17.cloned.1.call-start = ((), (), s32[]{:S(2)}) async-start(), calls=%async_computation.15 | async-start | bytes 9437184 | tf_op jit(solution)/shard_map/all_gather | solution.py:155
  302.9 348.0 %reduce-scatter.16.cloned.1.call-start = ((), (), s32[]{:S(2)}) async-start(), calls=%async_computation.18 | async-start | bytes 5242880 | tf_op jit(solution)/shard_map/reduce_scatter | solution.py:193
  574.6 76.4 %copy-start.1 = (bf16[2,128,2048]{2,1,0:T(8,128)(2,1)S(1)}, bf16[2,128,2048]{2,1,0:T(8,128)(2,1)}, u32[]{:S(2)}) copy-start(bf16[2,128,2048]{2,1,0:T(8,128)(2,1)} %reduce-scatter.12.cloned.1.call-done) | copy-start | bytes 3145732
  574.6 78.4 %copy-start.2 = (bf16[2,128,2048]{2,1,0:T(8,128)(2,1)S(1)}, bf16[2,128,2048]{2,1,0:T(8,128)(2,1)}, u32[]{:S(2)}) copy-start(bf16[2,128,2048]{2,1,0:T(8,128)(2,1)} %param.23) | copy-start | bytes 3145732
  574.6 163.0 %all-gather.21.cloned.1.call-start = ((), (), s32[]{:S(2)}) async-start(), calls=%async_computation.19 | async-start | bytes 5242880 | tf_op jit(solution)/shard_map/all_gather | solution.py:235
  656.2 255.1 %reduce-scatter.18.cloned.1.call-start = ((), (), s32[]{:S(2)}) async-start(), calls=%async_computation.20 | async-start | bytes 5242880 | tf_op jit(solution)/shard_map/reduce_scatter | solution.py:193
  835.9 150.7 %reduce-scatter.26.cloned.1.call-start = ((), (), s32[]{:S(2)}) async-start(), calls=%async_computation.24 | async-start | bytes 9437184 | tf_op jit(solution)/shard_map/reduce_scatter | solution.py:224
  850.5 180.4 %reduce-scatter.22.cloned.1.call-start = ((), (), s32[]{:S(2)}) async-start(), calls=%async_computation.22 | async-start | bytes 2359296 | tf_op jit(solution)/shard_map/reduce_scatter | solution.py:267
  856.8 223.6 %reduce-scatter.20.cloned.1.call-start = ((), (), s32[]{:S(2)}) async-start(), calls=%async_computation.21 | async-start | bytes 3538944 | tf_op jit(solution)/shard_map/reduce_scatter | solution.py:264
  864.7 294.6 %reduce-scatter.14.cloned.1.call-start = ((), (), s32[]{:S(2)}) async-start(), calls=%async_computation.16 | async-start | bytes 5242880 | tf_op jit(solution)/shard_map/reduce_scatter | solution.py:193
  878.8 420.7 %reduce-scatter.28.cloned.1.call-start = ((), (), s32[]{:S(2)}) async-start(), calls=%async_computation.25 | async-start | bytes 1081344
  914.6 501.1 %reduce-scatter.24.cloned.1.call-start = ((), (), s32[]{:S(2)}) async-start(), calls=%async_computation.23 | async-start | bytes 18874368 | tf_op jit(solution)/shard_map/reduce_scatter | solution.py:228
  1083.9 216.7 %copy-start.30 = (f32[64]{0:T(128)S(1)}, f32[64]{0:T(128)}, u32[]{:S(2)}) copy-start(f32[64]{0:T(128)} %param.27) | copy-start | bytes 772
  1083.9 216.7 %copy-start.32 = (f32[64]{0:T(128)S(1)}, f32[64]{0:T(128)}, u32[]{:S(2)}) copy-start(f32[64]{0:T(128)} %param.33) | copy-start | bytes 772
  1083.9 216.7 %copy-start.33 = (f32[64]{0:T(128)S(1)}, f32[64]{0:T(128)}, u32[]{:S(2)}) copy-start(f32[64]{0:T(128)} %param.39) | copy-start | bytes 772
  1083.9 217.3 %copy-start.31 = (f32[64]{0:T(128)S(1)}, f32[64]{0:T(128)}, u32[]{:S(2)}) copy-start(f32[64]{0:T(128)} %param.24) | copy-start | bytes 772
  1083.9 217.2 %copy-start.34 = (f32[64]{0:T(128)S(1)}, f32[64]{0:T(128)}, u32[]{:S(2)}) copy-start(f32[64]{0:T(128)} %param.30) | copy-start | bytes 772
  1083.9 217.2 %copy-start.35 = (f32[64]{0:T(128)S(1)}, f32[64]{0:T(128)}, u32[]{:S(2)}) copy-start(f32[64]{0:T(128)} %param.36) | copy-start | bytes 772
  1300.5 140.7 %copy-start.28 = (f32[64,1]{0,1:T(1,128)}, f32[64,1]{0,1:T(1,128)S(1)}, u32[]{:S(2)}) copy-start(f32[64,1]{0,1:T(1,128)S(1)} %copy.120) | copy-start | bytes 772
  1300.6 140.6 %copy-start.29 = (f32[64,1]{0,1:T(1,128)}, f32[64,1]{0,1:T(1,128)S(1)}, u32[]{:S(2)}) copy-start(f32[64,1]{0,1:T(1,128)S(1)} %copy.119) | copy-start | bytes 772
  (21 other events, 267.4 us)
Sparse Core Ops, SparseCore 0:
  10.5 34.9 all-gather.10
  84.1 76.9 all-gather.8
  163.6 26.5 all-gather.12
  204.4 74.9 reduce-scatter.11
  283.8 81.2 all-gather.14
  366.5 79.2 all-gather.18
  448.2 74.7 all-gather.16
  574.7 76.1 reduce-scatter.15
  656.3 81.2 all-gather.20
  836.0 75.2 reduce-scatter.17
  914.8 71.7 reduce-scatter.25
  989.7 41.0 reduce-scatter.21
  1034.2 46.0 reduce-scatter.19
  1082.5 76.7 reduce-scatter.13
  1162.0 137.4 reduce-scatter.27
  1302.9 112.6 reduce-scatter.23
